TPU v7x, 32 devices: a whole 2x2x4 slice. The times are simulated.
32 devices in a mesh: frame: 4 (over x, core), fsdp: 4 (over z), head: 2 (over y).
Axes of the slice: x: 2, y: 2, z: 4, core: 2. Of those that a mesh axis runs over, the one named last changes fastest.
Arguments:
- queries: bfloat16 [1024, 10240], P('frame', ('fsdp', 'head')), may hold values from -6 to 6
- noisy_keys: bfloat16 [1024, 10240], P('frame', ('fsdp', 'head')), may hold values from -6 to 6
- noisy_values: bfloat16 [1024, 10240], P('frame', ('fsdp', 'head')), may hold values from -6 to 6
- clean_keys: bfloat16 [1024, 10240], P('frame', ('fsdp', 'head')), may hold values from -10 to 10
- clean_values: bfloat16 [1024, 10240], P('frame', ('fsdp', 'head')), may hold values from -6 to 6
- gain_query: float32 [5120], replicated, may hold values from 0.5 to 2
- gain_key: float32 [5120], replicated, may hold values from 0.5 to 2
- out_grad: bfloat16 [1024, 10240], P('frame', ('fsdp', 'head')), may hold values from -6 to 6
Outputs:
- attended: bfloat16 [1024, 10240], P('frame', ('fsdp', 'head'))
- grad_queries: bfloat16 [1024, 10240], P('frame', ('fsdp', 'head'))
- grad_keys: bfloat16 [1024, 10240], P('frame', ('fsdp', 'head'))
- grad_values: bfloat16 [1024, 10240], P('frame', ('fsdp', 'head'))
- grad_gain_query: float32 [5120], replicated
- grad_gain_key: float32 [5120], replicated
All inputs are finite; a program needn't handle non-finite values.
Results may differ from a plain program's by a relative error of at most 0.012.
Values may be sent and summed in bfloat16 or wider, within the bound.
A program may use at most 64 MiB of HBM per device.

v0:
```python
import math
import jax
import jax.numpy as jnp
from jax import lax
from jax.sharding import PartitionSpec as P

D = 5120
DH = 128
EPSILON = 1e-06
MASKED = -1e30


def shifted(block, axis, distance):
    devices = range(lax.axis_size(axis))
    route = [((i - distance) % len(devices), i) for i in devices]
    return lax.ppermute(block, axis, route)


def project(left_side, right_side):
    return jnp.einsum("qhd,khd->hqk", left_side, right_side, preferred_element_type=jnp.float32)


def on_device(
    queries, noisy_keys, noisy_values, clean_keys, clean_values, gain_query, gain_key, out_grad
):
    length = queries.shape[0]
    width_dev = queries.shape[1]
    head_count = width_dev // DH
    scaling = 1.0 / math.sqrt(DH)
    own_frame = lax.axis_index("frame")
    own_start = own_frame * length
    pair_reach = lax.axis_size("fsdp") // 2
    half_index = lax.axis_index("fsdp") // pair_reach
    column_start = (half_index * lax.axis_size("head") + lax.axis_index("head")) * width_dev
    gain_q = lax.dynamic_slice_in_dim(gain_query, column_start, width_dev)
    gain_k = lax.dynamic_slice_in_dim(gain_key, column_start, width_dev)

    def with_partner(stats):
        other = shifted(stats, "fsdp", pair_reach)
        return stats + other

    q_full = queries.astype(jnp.float32)
    k_full = noisy_keys.astype(jnp.float32)
    squares_q, squares_k = lax.psum(
        (jnp.sum(q_full * q_full, axis=1), jnp.sum(k_full * k_full, axis=1)), "head"
    )
    squares = with_partner(jnp.stack([squares_q, squares_k]))
    rate_q = lax.rsqrt(squares[0] / D + EPSILON)
    rate_k = lax.rsqrt(squares[1] / D + EPSILON)
    normed_q = (
        (q_full * rate_q[:, None] * gain_q).astype(jnp.bfloat16).reshape(length, head_count, DH)
    )
    normed_k = (
        (k_full * rate_k[:, None] * gain_k).astype(jnp.bfloat16).reshape(length, head_count, DH)
    )
    values_own = noisy_values.reshape(length, head_count, DH)
    grads_out = out_grad.reshape(length, head_count, DH)
    own_scores = project(normed_q, normed_k) * scaling
    row_max = jnp.max(own_scores, axis=2)
    expo = jnp.exp(own_scores - row_max[:, :, None])
    totals = jnp.sum(expo, axis=2)
    summed = jnp.einsum(
        "hqk,khd->hqd", expo.astype(jnp.bfloat16), values_own, preferred_element_type=jnp.float32
    )

    def split_piece(portion):
        key_piece, value_piece = portion
        row_count = key_piece.shape[0]
        return (
            key_piece.reshape(row_count, head_count, DH),
            value_piece.reshape(row_count, head_count, DH),
            row_count,
        )

    def visible_scores(key_piece, row_count):
        scores = project(normed_q, key_piece) * scaling
        frame_of = jnp.arange(row_count, dtype=jnp.int32) // length
        return jnp.where((frame_of < own_frame)[None, None, :], scores, MASKED)

    initial = (row_max, totals, summed)
    key_piece, value_piece, row_count = split_piece(
        (
            lax.all_gather(clean_keys, "frame", axis=0, tiled=True),
            lax.all_gather(clean_values, "frame", axis=0, tiled=True),
        )
    )

    def attend(status):
        running, denominator, accumulated = status
        scores = visible_scores(key_piece, row_count)
        newest = jnp.maximum(running, jnp.max(scores, axis=2))
        exponent = jnp.exp(scores - newest[:, :, None])
        factor = jnp.exp(running - newest)
        added = jnp.einsum(
            "hqk,khd->hqd",
            exponent.astype(jnp.bfloat16),
            value_piece,
            preferred_element_type=jnp.float32,
        )
        return (
            newest,
            denominator * factor + jnp.sum(exponent, axis=2),
            accumulated * factor[:, :, None] + added,
        )

    running, denominator, accumulated = lax.cond(
        jnp.int32(0) < own_start, attend, lambda status: status, initial
    )
    log_total = running + jnp.log(denominator)
    output_f32 = accumulated / denominator[:, :, None]
    attended = jnp.transpose(output_f32, (1, 0, 2)).reshape(length, width_dev).astype(jnp.bfloat16)
    delta = jnp.sum(jnp.transpose(grads_out.astype(jnp.float32), (1, 0, 2)) * output_f32, axis=2)
    soft_probs = jnp.exp(own_scores - log_total[:, :, None])
    grad_probs = project(grads_out, values_own)
    grad_scores = (soft_probs * (grad_probs - delta[:, :, None])).astype(jnp.bfloat16)
    grad_qn = (
        jnp.einsum("hqk,khd->qhd", grad_scores, normed_k, preferred_element_type=jnp.float32)
        * scaling
    )
    grad_kn = (
        jnp.einsum("hqk,qhd->khd", grad_scores, normed_q, preferred_element_type=jnp.float32)
        * scaling
    )
    grad_vv = jnp.einsum(
        "hqk,qhd->khd",
        soft_probs.astype(jnp.bfloat16),
        grads_out,
        preferred_element_type=jnp.float32,
    )
    reflect_key_piece, reflect_value_piece, reflect_row_count = split_piece(
        (
            lax.all_gather(clean_keys, "frame", axis=0, tiled=True),
            lax.all_gather(clean_values, "frame", axis=0, tiled=True),
        )
    )

    def attend_back(current):
        scores = visible_scores(reflect_key_piece, reflect_row_count)
        piece_probs = jnp.exp(scores - log_total[:, :, None])
        piece_grads = project(grads_out, reflect_value_piece)
        weighted = (piece_probs * (piece_grads - delta[:, :, None])).astype(jnp.bfloat16)
        return (
            current
            + jnp.einsum(
                "hqk,khd->qhd", weighted, reflect_key_piece, preferred_element_type=jnp.float32
            )
            * scaling
        )

    grad_qn = lax.cond(jnp.int32(0) < own_start, attend_back, lambda current: current, grad_qn)
    plain_q = grad_qn.reshape(length, width_dev)
    plain_k = grad_kn.reshape(length, width_dev)
    flat_q = plain_q * gain_q
    flat_k = plain_k * gain_k
    inner_q, inner_k = lax.psum(
        (jnp.sum(q_full * flat_q, axis=1), jnp.sum(k_full * flat_k, axis=1)), "head"
    )
    inners = with_partner(jnp.stack([inner_q, inner_k]))
    cube_q = rate_q * rate_q * rate_q * inners[0] / D
    cube_k = rate_k * rate_k * rate_k * inners[1] / D
    grad_queries = (rate_q[:, None] * flat_q - q_full * cube_q[:, None]).astype(jnp.bfloat16)
    grad_keys = (rate_k[:, None] * flat_k - k_full * cube_k[:, None]).astype(jnp.bfloat16)
    part_q = jnp.sum(plain_q * q_full * rate_q[:, None], axis=0)
    part_k = jnp.sum(plain_k * k_full * rate_k[:, None], axis=0)
    blank = jnp.zeros((D,), jnp.float32)
    spread_q = lax.dynamic_update_slice_in_dim(blank, part_q, column_start, 0)
    spread_k = lax.dynamic_update_slice_in_dim(blank, part_k, column_start, 0)
    grad_gain_query, grad_gain_key = lax.psum((spread_q, spread_k), ("frame", "fsdp", "head"))
    grad_values = grad_vv.reshape(length, width_dev).astype(jnp.bfloat16)
    return (attended, grad_queries, grad_keys, grad_values, grad_gain_query, grad_gain_key)


def solution(mesh):
    placed = (
        P("frame", ("fsdp", "head")),
        P("frame", ("fsdp", "head")),
        P("frame", ("fsdp", "head")),
        P("frame", ("fsdp", "head")),
        P("frame", ("fsdp", "head")),
        P(),
        P(),
        P("frame", ("fsdp", "head")),
    )
    return jax.shard_map(
        on_device,
        mesh=mesh,
        in_specs=placed,
        out_specs=(
            P("frame", ("fsdp", "head")),
            P("frame", ("fsdp", "head")),
            P("frame", ("fsdp", "head")),
            P("frame", ("fsdp", "head")),
            P(),
            P(),
        ),
        check_vma=False,
    )
```

profile of v0, /device:TPU:0, one launch (start us, length us, event | category | flops | bytes accessed | tf_op | source)
XLA Modules:
  0.0 166.8 jit_solution(3588407405975726999)
XLA Ops:
  7.2 0.0 all-gather.3.cloned.1.call-start
  7.2 0.7 all-gather.3.cloned.1.call-update
  7.9 0.0 all-gather.5.cloned.1.call-start
  8.0 2.2 %copy.46 = bf16[256,1280]{0,1:T(8,128)(2,1)} copy(bf16[256,1280]{1,0:T(8,128)(2,1)} %param.16) | data formatting | bytes 1310720 | tf_op args[4]
  10.1 0.0 all-gather.5.cloned.1.call-update
  10.2 0.0 copy-start.20
  10.2 0.2 copy.38
  10.4 0.2 copy.39
  10.7 0.2 fusion.38
  10.9 0.2 fusion.46
  11.1 5.9 %all-reduce.2 = (f32[1,256]{1,0:T(1,128)S(1)}, f32[1,256]{1,0:T(1,128)S(1)}) all-reduce(f32[1,256]{1,0:T(1,128)S(1)} %bitcast.86, f32[1,256]{1,0:T(1,128)S(1)} %bitcast.85), channel_id=1, replica_groups=mesh['frame'=4,'fsdp'=4,'head'=2] {'head'}, use_global_device_ids=true, to_apply=%region_3.4 | all-reduce | flops 512 | bytes 4096 | tf_op jit(solution)/shard_map/psum | solution.py:44
  17.0 3.2 %collective-permute-start = (f32[2,256]{1,0:T(2,128)S(1)}, f32[2,256]{1,0:T(2,128)S(1)}, u32[]{:S(2)}, u32[]{:S(2)}) collective-permute-start(f32[2,256]{1,0:T(2,128)S(1)} %pad_maximum_fusion), channel_id=1, source_target_pairs={{4,0},{6,2},{0,4},{2,6},{5,1},{7,3},{1,5},{3,7},{12,8},{14,10},{8,... | collective-permute-start | bytes 6152 | tf_op jit(solution)/shard_map/ppermute | solution.py:16
  20.2 0.8 dynamic_slice.6
  20.9 0.8 dynamic_slice.7
  21.7 1.1 copy.42
  22.8 1.1 copy.51
  23.9 0.2 fusion.40
  24.2 0.2 fusion.48
  24.4 0.0 copy-start.9
  24.4 0.6 multiply_reduce_fusion
  25.0 0.3 copy-done.11
  25.3 0.4 fusion.32
  25.8 0.0 copy-done.9
  25.8 1.8 %fusion.36 = f32[10,256,128]{2,1,0:T(8,128)} fusion(bf16[256,10,128]{0,2,1:T(8,128)(2,1)S(1)} %bitcast.69, f32[10,256,256]{1,2,0:T(8,128)S(1)} %get-tuple-element.167, f32[10,256]{1,0:T(8,128)S(1)} %get-tuple-element.166), kind=kOutput, calls=%fused_computation.61 | convolution fusion | flops 169738240 | bytes 4597760 | tf_op jit(solution)/shard_map/hqk,khd->hqd/dot_general | solution.py:62
  27.6 10.3 %all-gather.3.cloned.1.call-done = bf16[1024,1280]{1,0:T(8,128)(2,1)} async-done(((bf16[256,1280]{1,0:T(8,128)(2,1)}), bf16[1024,1280]{1,0:T(8,128)(2,1)}) %all-gather.3.cloned.1.call-update) | async-done | bytes 2621456 | tf_op jit(solution)/shard_map/all_gather | solution.py:83
  37.9 4.5 %copy.45 = bf16[1024,1280]{0,1:T(8,128)(2,1)} copy(bf16[1024,1280]{1,0:T(8,128)(2,1)} %all-gather.3.cloned.1.call-done) | data formatting | bytes 5242880 | tf_op jit(solution)/shard_map/all_gather | solution.py:83
  42.4 23.5 %all-gather.5.cloned.1.call-done = bf16[1024,1280]{0,1:T(8,128)(2,1)} async-done(((bf16[256,1280]{0,1:T(8,128)(2,1)}), bf16[1024,1280]{0,1:T(8,128)(2,1)}) %all-gather.5.cloned.1.call-update) | async-done | bytes 2621456 | tf_op jit(solution)/shard_map/all_gather | solution.py:84
  65.9 2.8 %copy.50 = f32[10,256,128]{1,2,0:T(8,128)} copy(f32[10,256,128]{2,1,0:T(8,128)} %get-tuple-element.144) | data formatting | bytes 2621440 | tf_op jit(solution)/shard_map/cond | solution.py:106
  68.7 2.7 %convolution_convert_fusion = bf16[10,256,128]{1,2,0:T(8,128)(2,1)} fusion(bf16[256,10,128]{0,2,1:T(8,128)(2,1)} %bitcast.65, f32[10,256,256]{1,2,0:T(8,128)S(1)} %get-tuple-element.167, f32[10,256]{1,0:T(8,128)S(1)} %log_add_fusion), kind=kOutput, calls=%fused_computation.60 | convolution fusion | flops 170065920 | bytes 3942400 | tf_op jit(solution)/shard_map/hqk,qhd->khd/dot_general | solution.py:124
  71.5 1.1 fusion.54
  72.5 0.8 multiply_convert_fusion.8
  73.3 0.3 copy-done.12
  73.6 1.4 fusion.34
  75.0 0.6 convolution_multiply_fusion
  75.6 0.7 fusion.53
  76.3 0.9 copy-done
  77.3 2.1 %fusion.45 = (f32[1280]{0:T(1024)S(1)}, f32[256]{0:T(256)S(1)}) fusion(f32[256,1280]{0,1:T(8,128)} %get-tuple-element.92, bf16[256,1280]{0,1:T(8,128)(2,1)S(1)} %copy.38, f32[256]{0:T(256)S(1)} %bitcast.76, f32[1280]{0:T(1024)S(1)} %dynamic_slice.6), kind=kLoop, calls=%fused_computation.69 | loop fusion | flops 2292224 | bytes 1978368 | tf_op jit(solution)/shard_map/reduce_sum | solution.py:163
  79.4 4.9 %all-reduce.1 = (f32[1,256]{1,0:T(1,128)S(1)}, f32[1,256]{1,0:T(1,128)S(1)}) all-reduce(f32[1,256]{1,0:T(1,128)S(1)} %bitcast.83, f32[1,256]{1,0:T(1,128)S(1)} %bitcast.84), channel_id=1, replica_groups=mesh['frame'=4,'fsdp'=4,'head'=2] {'head'}, use_global_device_ids=true, to_apply=%region_16.17 | all-reduce | flops 512 | bytes 4096 | tf_op jit(solution)/shard_map/psum | solution.py:155
  84.3 2.5 %collective-permute-start.1 = (f32[2,256]{1,0:T(2,128)S(1)}, f32[2,256]{1,0:T(2,128)S(1)}, u32[]{:S(2)}, u32[]{:S(2)}) collective-permute-start(f32[2,256]{1,0:T(2,128)S(1)} %pad_maximum_fusion.1), channel_id=1, source_target_pairs={{4,0},{6,2},{0,4},{2,6},{5,1},{7,3},{1,5},{3,7},{12,8},{14,10},{8,... | collective-permute-start | bytes 6152 | tf_op jit(solution)/shard_map/ppermute | solution.py:16
  86.8 0.2 dynamic_update_slice.7
  87.0 0.3 dynamic_update_slice.6
  87.3 65.2 %all-reduce = (f32[5120]{0:T(1024)}, f32[5120]{0:T(1024)}) all-reduce(f32[5120]{0:T(1024)S(1)} %dynamic_update_slice.6, f32[5120]{0:T(1024)S(1)} %dynamic_update_slice.7), channel_id=1, replica_groups=mesh['frame'=4,'fsdp'=4,'head'=2] {'frame','fsdp','head'}, use_global_device_ids=true, to_apply=%region_18.19 | all-reduce | flops 10240 | bytes 81920 | tf_op jit(solution)/shard_map/psum | solution.py:168
  152.6 2.2 %copy.64 = bf16[256,1280]{1,0:T(8,128)(2,1)} copy(bf16[256,1280]{0,1:T(8,128)(2,1)} %bitcast.74) | data formatting | bytes 1310720
  154.8 1.1 copy.61
  155.9 0.3 fusion.51
  156.2 1.1 copy.63
  157.3 1.6 fusion.43
  158.9 1.1 copy.62
  (47 shorter events, 0.2 us)
Async XLA Ops:
  7.2 3.0 %copy-start.17 = (bf16[256,1280]{1,0:T(8,128)(2,1)S(1)}, bf16[256,1280]{1,0:T(8,128)(2,1)}, u32[]{:S(2)}) copy-start(bf16[256,1280]{1,0:T(8,128)(2,1)} %param.12) | copy-start | bytes 1966084
  7.2 3.2 %copy-start.18 = (bf16[256,1280]{1,0:T(8,128)(2,1)S(1)}, bf16[256,1280]{1,0:T(8,128)(2,1)}, u32[]{:S(2)}) copy-start(bf16[256,1280]{1,0:T(8,128)(2,1)} %param.13) | copy-start | bytes 1966084
  7.2 30.7 %all-gather.3.cloned.1.call-start = ((), (), s32[]{:S(2)}) async-start(), calls=%async_computation | async-start | bytes 3276800 | tf_op jit(solution)/shard_map/all_gather | solution.py:83
  7.9 58.0 %all-gather.5.cloned.1.call-start = ((), (), s32[]{:S(2)}) async-start(), calls=%async_computation.1 | async-start | bytes 3276800 | tf_op jit(solution)/shard_map/all_gather | solution.py:84
  10.1 11.6 %copy-start.19 = (bf16[256,1280]{1,0:T(8,128)(2,1)S(1)}, bf16[256,1280]{1,0:T(8,128)(2,1)}, u32[]{:S(2)}) copy-start(bf16[256,1280]{1,0:T(8,128)(2,1)} %param.14) | copy-start | bytes 1966084
  10.2 12.6 %copy-start.20 = (bf16[256,1280]{1,0:T(8,128)(2,1)S(1)}, bf16[256,1280]{1,0:T(8,128)(2,1)}, u32[]{:S(2)}) copy-start(bf16[256,1280]{1,0:T(8,128)(2,1)} %param.19) | copy-start | bytes 1966084
  10.7 13.5 %copy-start.1 = (bf16[256,1280]{0,1:T(8,128)(2,1)}, bf16[256,1280]{0,1:T(8,128)(2,1)S(1)}, u32[]{:S(2)}) copy-start(bf16[256,1280]{0,1:T(8,128)(2,1)S(1)} %copy.39) | copy-start | bytes 1966084
  17.0 6.9 %collective-permute-start = (f32[2,256]{1,0:T(2,128)S(1)}, f32[2,256]{1,0:T(2,128)S(1)}, u32[]{:S(2)}, u32[]{:S(2)}) collective-permute-start(f32[2,256]{1,0:T(2,128)S(1)} %pad_maximum_fusion), channel_id=1, source_target_pairs={{4,0},{6,2},{0,4},{2,6},{5,1},{7,3},{1,5},{3,7},{12,8},{14,10},{8,... | collective-permute-start | bytes 6152 | tf_op jit(solution)/shard_map/ppermute | solution.py:16
  24.2 0.9 copy-start.4
  24.4 0.9 copy-start.11
  24.4 1.4 copy-start.9
  68.7 2.8 %copy-start.8 = (bf16[256,1280]{0,1:T(8,128)(2,1)S(1)}, bf16[256,1280]{0,1:T(8,128)(2,1)}, u32[]{:S(2)}) copy-start(bf16[256,1280]{0,1:T(8,128)(2,1)} %copy.51) | copy-start | bytes 1966084
  68.7 2.8 %copy-start.13 = (f32[10,256,128]{1,2,0:T(8,128)S(1)}, f32[10,256,128]{1,2,0:T(8,128)}, u32[]{:S(2)}) copy-start(f32[10,256,128]{1,2,0:T(8,128)} %copy.50) | copy-start | bytes 3932164
  68.7 3.8 %copy-start.10 = (bf16[256,1280]{0,1:T(8,128)(2,1)S(1)}, bf16[256,1280]{0,1:T(8,128)(2,1)}, u32[]{:S(2)}) copy-start(bf16[256,1280]{0,1:T(8,128)(2,1)} %copy.42) | copy-start | bytes 1966084
  72.5 1.1 copy-start.12
  73.6 1.4 copy-start.5
  73.6 2.0 %copy-start.2 = (bf16[256,1280]{0,1:T(8,128)(2,1)S(1)}, bf16[256,1280]{0,1:T(8,128)(2,1)}, u32[]{:S(2)}) copy-start(bf16[256,1280]{0,1:T(8,128)(2,1)} %copy-done.1) | copy-start | bytes 1966084
  75.0 2.2 %copy-start = (bf16[1024,1280]{0,1:T(8,128)(2,1)S(1)}, bf16[1024,1280]{0,1:T(8,128)(2,1)}, u32[]{:S(2)}) copy-start(bf16[1024,1280]{0,1:T(8,128)(2,1)} %copy.45) | copy-start | bytes 7864324
  75.6 1.6 copy-start.6
  77.3 77.5 %copy-start.16 = (bf16[10,256,128]{1,2,0:T(8,128)(2,1)S(1)}, bf16[10,256,128]{1,2,0:T(8,128)(2,1)}, u32[]{:S(2)}) copy-start(bf16[10,256,128]{1,2,0:T(8,128)(2,1)} %get-tuple-element.161) | copy-start | bytes 1966084
  77.3 78.6 %copy-start.3 = (bf16[256,1280]{0,1:T(8,128)(2,1)S(1)}, bf16[256,1280]{0,1:T(8,128)(2,1)}, u32[]{:S(2)}) copy-start(bf16[256,1280]{0,1:T(8,128)(2,1)} %copy-done.1) | copy-start | bytes 1966084
  77.3 78.6 %copy-start.7 = (f32[10,128,256]{2,1,0:T(8,128)S(1)}, f32[10,128,256]{2,1,0:T(8,128)}, u32[]{:S(2)}) copy-start(f32[10,128,256]{2,1,0:T(8,128)} %copy-done.6) | copy-start | bytes 3932164
  84.3 71.5 %collective-permute-start.1 = (f32[2,256]{1,0:T(2,128)S(1)}, f32[2,256]{1,0:T(2,128)S(1)}, u32[]{:S(2)}, u32[]{:S(2)}) collective-permute-start(f32[2,256]{1,0:T(2,128)S(1)} %pad_maximum_fusion.1), channel_id=1, source_target_pairs={{4,0},{6,2},{0,4},{2,6},{5,1},{7,3},{1,5},{3,7},{12,8},{14,10},{8,... | collective-permute-start | bytes 6152 | tf_op jit(solution)/shard_map/ppermute | solution.py:16
Sparse Core Ops, SparseCore 0:
  9.6 28.2 all-gather.2
  40.0 25.8 all-gather.4
where the time goes:
time: 167 us
  blocking collectives  76.1 us (46%)
  waiting for transfers between devices  34.5 us (21%)
  local copies, waits for them, and re-layouts  21.2 us (13%)
  between operations  14.3 us (9%)
  matrix products  7.9 us (5%)
  other arithmetic  7.13 us (4%)
  starting transfers between devices  5.7 us (3%)
    psum x1, blocking collectives, on_device(): lax.psum((spread_q, spread_k), ('frame', 'fsdp', 'head'))  65.2 us
    all_gather x1, waiting for transfers between devices, on_device(): lax.all_gather(clean_values, 'frame', axis=0, tiled=True)  23.5 us
    unnamed x47, local copies, waits for them, and re-layouts  11.8 us
    all_gather x1, waiting for transfers between devices, on_device(): lax.all_gather(clean_keys, 'frame', axis=0, tiled=True)  10.3 us
    psum x1, blocking collectives, on_device(): lax.psum((jnp.sum(q_full * q_full, axis=1), jnp.sum(k_full * k_full, axis...  5.89 us
    ppermute x2, starting transfers between devices, shifted(): return lax.ppermute(block, axis, route)  5.62 us
    psum x1, blocking collectives, on_device(): lax.psum((jnp.sum(q_full * flat_q, axis=1), jnp.sum(k_full * flat_k, axis...  4.93 us
    all_gather x1, local copies, waits for them, and re-layouts, on_device(): lax.all_gather(clean_keys, 'frame', axis=0, tiled=True)  4.54 us
  transfers between devices with their start and end apart: 4, of which 2 were waited for; matrix products, arithmetic and copies ran while one was open for 11% of the time, Pallas kernels for 0%

commit v1 on v0

--- a/solution.py
+++ b/solution.py
@@ -8,6 +8,24 @@
 DH = 128
 EPSILON = 1e-06
 MASKED = -1e30
+
+
+def collect(array, axis, dim):
+    ways, here, hop = (lax.axis_size(axis), lax.axis_index(axis), array.shape[dim])
+    dims = [n * ways if d == dim else n for d, n in enumerate(array.shape)]
+    full = lax.dynamic_update_slice_in_dim(
+        jnp.zeros(dims, array.dtype), array, here * hop, axis=dim
+    )
+    going_up = going_down = array
+    for far in range(1, ways // 2 + 1):
+        going_up = lax.ppermute(going_up, axis, [(d, (d + 1) % ways) for d in range(ways)])
+        full = lax.dynamic_update_slice_in_dim(full, going_up, (here - far) % ways * hop, axis=dim)
+        if 2 * far < ways:
+            going_down = lax.ppermute(going_down, axis, [(d, (d - 1) % ways) for d in range(ways)])
+            full = lax.dynamic_update_slice_in_dim(
+                full, going_down, (here + far) % ways * hop, axis=dim
+            )
+    return full
 
 
 def shifted(block, axis, distance):
@@ -79,10 +97,7 @@
 
     initial = (row_max, totals, summed)
     key_piece, value_piece, row_count = split_piece(
-        (
-            lax.all_gather(clean_keys, "frame", axis=0, tiled=True),
-            lax.all_gather(clean_values, "frame", axis=0, tiled=True),
-        )
+        (lax.all_gather(clean_keys, "frame", axis=0, tiled=True), collect(clean_values, "frame", 0))
     )
 
     def attend(status):

time: 167 us -> 175 us (1.048)
  waiting for transfers between devices: 34.5 us -> 23.7 us
  starting transfers between devices: 5.7 us -> 15.2 us
  blocking collectives: 76.1 us -> 82.1 us
  other arithmetic: 7.13 us -> 10 us
    all_gather x1, waiting for transfers between devices: 23.5 us -> 12.2 us  [on_device(): lax.all_gather(clean_values, 'frame', axis=0, tiled=True)]
    ppermute x0 -> x3, starting transfers between devices: none -> 9.51 us  [the longest x2 7.59 us: collect(): lax.ppermute(going_up, axis, [(d, (d + 1) % ways) for d in range(ways)])]
    psum x1, blocking collectives: 65.2 us -> 71.9 us  [on_device(): lax.psum((spread_q, spread_k), ('frame', 'fsdp', 'head'))]
    unnamed x47 -> x37, local copies, waits for them, and re-layouts: 11.8 us -> 11.7 us
  transfers between devices with their start and end apart: 4 -> 7, of which waited for: 2 -> 3; matrix products, arithmetic and copies ran while one was open for 11% -> 17% of each run, Pallas kernels for 0% -> 0%
where the time goes in v1:
time: 175 us; the launch traced here: 174 us
  blocking collectives  82.1 us (47%)
  waiting for transfers between devices  23.7 us (14%)
  local copies, waits for them, and re-layouts  21.1 us (12%)
  starting transfers between devices  15.2 us (9%)
  between operations  14.3 us (8%)
  other arithmetic  10 us (6%)
  matrix products  7.69 us (4%)
    psum x1, blocking collectives, on_device(): lax.psum((spread_q, spread_k), ('frame', 'fsdp', 'head'))  71.9 us
    all_gather x1, waiting for transfers between devices, on_device(): lax.all_gather(clean_values, 'frame', axis=0, tiled=True)  12.2 us
    unnamed x37, local copies, waits for them, and re-layouts  11.7 us
    all_gather x1, waiting for transfers between devices, on_device(): lax.all_gather(clean_keys, 'frame', axis=0, tiled=True)  9.34 us
    ppermute x2, starting transfers between devices, collect(): lax.ppermute(going_up, axis, [(d, (d + 1) % ways) for d in range(ways)])  7.59 us
    ppermute x2, starting transfers between devices, shifted(): return lax.ppermute(block, axis, route)  5.62 us
    psum x1, blocking collectives, on_device(): lax.psum((jnp.sum(q_full * q_full, axis=1), jnp.sum(k_full * k_full, axis...  5.23 us
    psum x1, blocking collectives, on_device(): lax.psum((jnp.sum(q_full * flat_q, axis=1), jnp.sum(k_full * flat_k, axis...  4.93 us
  transfers between devices with their start and end apart: 7, of which 3 were waited for; matrix products, arithmetic and copies ran while one was open for 17% of the time, Pallas kernels for 0%

profile of v1, /device:TPU:0, one launch (start us, length us, event | category | flops | bytes accessed | tf_op | source)
XLA Modules:
  0.0 174.2 jit_solution(7409436228303800966)
XLA Ops:
  7.2 0.0 all-gather.3.cloned.1.call-start
  7.2 0.7 all-gather.3.cloned.1.call-update
  7.9 0.0 all-gather.5.cloned.1.call-start
  8.0 2.2 %copy.46 = bf16[256,1280]{0,1:T(8,128)(2,1)} copy(bf16[256,1280]{1,0:T(8,128)(2,1)} %param.16) | data formatting | bytes 1310720 | tf_op args[4]
  10.1 0.5 collective-permute-start.1
  10.6 1.9 %collective-permute-start.2 = (bf16[256,1280]{0,1:T(8,128)(2,1)}, bf16[256,1280]{0,1:T(8,128)(2,1)}, u32[]{:S(2)}, u32[]{:S(2)}) collective-permute-start(bf16[256,1280]{0,1:T(8,128)(2,1)} %copy.46), channel_id=1, source_target_pairs={{0,24},{8,0},{16,8},{24,16},{1,25},{9,1},{17,9},{25,17},{2,26},{10... | collective-permute-start | bytes 1966088 | tf_op jit(solution)/shard_map/ppermute | solution.py:24
  12.5 1.3 copy.38
  13.9 0.2 copy.39
  14.1 0.2 fusion.38
  14.3 0.2 fusion.46
  14.5 5.2 %all-reduce.2 = (f32[1,256]{1,0:T(1,128)S(1)}, f32[1,256]{1,0:T(1,128)S(1)}) all-reduce(f32[1,256]{1,0:T(1,128)S(1)} %bitcast.90, f32[1,256]{1,0:T(1,128)S(1)} %bitcast.89), channel_id=1, replica_groups=mesh['frame'=4,'fsdp'=4,'head'=2] {'head'}, use_global_device_ids=true, to_apply=%region_3.4 | all-reduce | flops 512 | bytes 4096 | tf_op jit(solution)/shard_map/psum | solution.py:62
  19.8 3.2 %collective-permute-start = (f32[2,256]{1,0:T(2,128)S(1)}, f32[2,256]{1,0:T(2,128)S(1)}, u32[]{:S(2)}, u32[]{:S(2)}) collective-permute-start(f32[2,256]{1,0:T(2,128)S(1)} %pad_maximum_fusion), channel_id=1, source_target_pairs={{4,0},{6,2},{0,4},{2,6},{5,1},{7,3},{1,5},{3,7},{12,8},{14,10},{8,... | collective-permute-start | bytes 6152 | tf_op jit(solution)/shard_map/ppermute | solution.py:34
  23.0 0.8 dynamic_slice.7
  23.8 0.8 dynamic_slice.6
  24.6 1.1 copy.42
  25.6 1.1 copy.52
  26.8 0.2 fusion.48
  27.0 0.2 fusion.40
  27.3 1.4 collective-permute-done.1
  28.7 7.1 %collective-permute-start.3 = (bf16[256,1280]{0,1:T(8,128)(2,1)}, bf16[256,1280]{0,1:T(8,128)(2,1)}, u32[]{:S(2)}, u32[]{:S(2)}) collective-permute-start(bf16[256,1280]{0,1:T(8,128)(2,1)} %collective-permute-done.1), channel_id=1, source_target_pairs={{0,8},{8,16},{16,24},{24,0},{1,9},{9,17},{17,25},{25,1},{2,10},{10... | collective-permute-start | bytes 1966088 | tf_op jit(solution)/shard_map/ppermute | solution.py:21
  35.8 0.6 multiply_reduce_fusion
  36.4 0.4 fusion.32
  36.8 0.1 copy-done.7
  36.9 1.8 %fusion.36 = f32[10,256,128]{2,1,0:T(8,128)} fusion(bf16[256,10,128]{0,2,1:T(8,128)(2,1)S(1)} %bitcast.72, f32[10,256,256]{1,2,0:T(8,128)S(1)} %get-tuple-element.444, f32[10,256]{1,0:T(8,128)S(1)} %get-tuple-element.443), kind=kOutput, calls=%fused_computation.64 | convolution fusion | flops 169738240 | bytes 4597760 | tf_op jit(solution)/shard_map/hqk,khd->hqd/dot_general | solution.py:80
  38.7 9.3 %all-gather.3.cloned.1.call-done = bf16[1024,1280]{1,0:T(8,128)(2,1)} async-done(((bf16[256,1280]{1,0:T(8,128)(2,1)}), bf16[1024,1280]{1,0:T(8,128)(2,1)}) %all-gather.3.cloned.1.call-update) | async-done | bytes 2621456 | tf_op jit(solution)/shard_map/all_gather | solution.py:100
  48.0 4.5 %copy.45 = bf16[1024,1280]{0,1:T(8,128)(2,1)} copy(bf16[1024,1280]{1,0:T(8,128)(2,1)} %all-gather.3.cloned.1.call-done) | data formatting | bytes 5242880 | tf_op jit(solution)/shard_map/all_gather | solution.py:100
  52.5 0.2 conditional.2
  52.7 2.8 %copy.51 = f32[10,256,128]{1,2,0:T(8,128)} copy(f32[10,256,128]{2,1,0:T(8,128)} %get-tuple-element.421) | data formatting | bytes 2621440 | tf_op jit(solution)/shard_map/cond | solution.py:121
  55.5 2.8 %fusion.54 = (f32[10,256]{1,0:T(8,128)S(1)}, bf16[10,256,128]{1,2,0:T(8,128)(2,1)}) fusion(bf16[256,10,128]{0,2,1:T(8,128)(2,1)} %bitcast.68, f32[10,256,128]{1,2,0:T(8,128)} %copy.51, f32[10,256]{1,0:T(8,128)S(1)} %get-tuple-element.420), kind=kLoop, calls=%fused_computation.83 | loop fusion | flops 1635840 | bytes 2641920 | tf_op jit(solution)/shard_map/reduce_sum | solution.py:127
  58.3 0.8 multiply_convert_fusion.8
  59.1 0.3 copy-done.10
  59.4 1.4 fusion.34
  60.8 1.6 convolution_multiply_fusion
  62.4 1.5 convolution_convert_fusion
  63.9 12.2 %all-gather.5.cloned.1.call-done = bf16[1024,1280]{0,1:T(8,128)(2,1)} async-done(((bf16[256,1280]{0,1:T(8,128)(2,1)}), bf16[1024,1280]{0,1:T(8,128)(2,1)}) %all-gather.5.cloned.1.call-update) | async-done | bytes 2621456 | tf_op jit(solution)/shard_map/all_gather | solution.py:148
  76.2 2.1 %fusion.45 = (f32[1280]{0:T(1024)S(1)}, f32[256]{0:T(256)S(1)}) fusion(f32[256,1280]{0,1:T(8,128)} %get-tuple-element.330, bf16[256,1280]{0,1:T(8,128)(2,1)S(1)} %copy.38, f32[256]{0:T(256)S(1)} %bitcast.80, f32[1280]{0:T(1024)S(1)} %dynamic_slice.6), kind=kLoop, calls=%fused_computation.72 | loop fusion | flops 2292224 | bytes 1978368 | tf_op jit(solution)/shard_map/reduce_sum | solution.py:178
  78.3 1.8 %fusion.53 = (f32[1280]{0:T(1024)S(1)}, f32[256]{0:T(256)S(1)}) fusion(bf16[256,1280]{0,1:T(8,128)(2,1)} %copy-done.1, f32[10,128,256]{2,1,0:T(8,128)S(1)} %copy-done.5, f32[256]{0:T(256)S(1)} %bitcast.84, f32[1280]{0:T(1024)S(1)} %dynamic_slice.7), kind=kLoop, calls=%fused_computation.80 | loop fusion | flops 2292224 | bytes 1978368 | tf_op jit(solution)/shard_map/reduce_sum | solution.py:179
  80.2 4.9 %all-reduce.1 = (f32[1,256]{1,0:T(1,128)S(1)}, f32[1,256]{1,0:T(1,128)S(1)}) all-reduce(f32[1,256]{1,0:T(1,128)S(1)} %bitcast.88, f32[1,256]{1,0:T(1,128)S(1)} %bitcast.87), channel_id=1, replica_groups=mesh['frame'=4,'fsdp'=4,'head'=2] {'head'}, use_global_device_ids=true, to_apply=%region_16.17 | all-reduce | flops 512 | bytes 4096 | tf_op jit(solution)/shard_map/psum | solution.py:170
  85.1 2.5 %collective-permute-start.4 = (f32[2,256]{1,0:T(2,128)S(1)}, f32[2,256]{1,0:T(2,128)S(1)}, u32[]{:S(2)}, u32[]{:S(2)}) collective-permute-start(f32[2,256]{1,0:T(2,128)S(1)} %pad_maximum_fusion.1), channel_id=1, source_target_pairs={{4,0},{6,2},{0,4},{2,6},{5,1},{7,3},{1,5},{3,7},{12,8},{14,10},{8,... | collective-permute-start | bytes 6152 | tf_op jit(solution)/shard_map/ppermute | solution.py:34
  87.6 0.2 dynamic_update_slice.38
  87.8 0.3 dynamic_update_slice.39
  88.1 71.9 %all-reduce = (f32[5120]{0:T(1024)}, f32[5120]{0:T(1024)}) all-reduce(f32[5120]{0:T(1024)S(1)} %dynamic_update_slice.38, f32[5120]{0:T(1024)S(1)} %dynamic_update_slice.39), channel_id=1, replica_groups=mesh['frame'=4,'fsdp'=4,'head'=2] {'frame','fsdp','head'}, use_global_device_ids=true, to_apply=%region_18.19 | all-reduce | flops 10240 | bytes 81920 | tf_op jit(solution)/shard_map/psum | solution.py:183
  160.0 2.2 %copy.65 = bf16[256,1280]{1,0:T(8,128)(2,1)} copy(bf16[256,1280]{0,1:T(8,128)(2,1)} %bitcast.78) | data formatting | bytes 1310720
  162.2 1.1 copy.62
  163.3 0.3 fusion.51
  163.6 1.1 copy.64
  164.7 1.6 fusion.43
  166.3 1.1 copy.63
  (43 shorter events, 0.2 us)
Async XLA Ops:
  7.2 6.7 %copy-start.15 = (bf16[256,1280]{1,0:T(8,128)(2,1)S(1)}, bf16[256,1280]{1,0:T(8,128)(2,1)}, u32[]{:S(2)}) copy-start(bf16[256,1280]{1,0:T(8,128)(2,1)} %param.13) | copy-start | bytes 1966084
  7.2 40.8 %all-gather.3.cloned.1.call-start = ((), (), s32[]{:S(2)}) async-start(), calls=%async_computation | async-start | bytes 3276800 | tf_op jit(solution)/shard_map/all_gather | solution.py:100
  7.9 68.3 %all-gather.5.cloned.1.call-start = ((), (), s32[]{:S(2)}) async-start(), calls=%async_computation.1 | async-start | bytes 3276800 | tf_op jit(solution)/shard_map/all_gather | solution.py:148
  10.1 14.4 %copy-start.16 = (bf16[256,1280]{1,0:T(8,128)(2,1)S(1)}, bf16[256,1280]{1,0:T(8,128)(2,1)}, u32[]{:S(2)}) copy-start(bf16[256,1280]{1,0:T(8,128)(2,1)} %param.14) | copy-start | bytes 1966084
  10.1 18.5 %collective-permute-start.1 = (bf16[256,1280]{0,1:T(8,128)(2,1)}, bf16[256,1280]{0,1:T(8,128)(2,1)}, u32[]{:S(2)}, u32[]{:S(2)}) collective-permute-start(bf16[256,1280]{0,1:T(8,128)(2,1)} %copy.46), channel_id=1, source_target_pairs={{0,8},{8,16},{16,24},{24,0},{1,9},{9,17},{17,25},{25,1},{2,10},{10... | collective-permute-start | bytes 1966088 | tf_op jit(solution)/shard_map/ppermute | solution.py:21
  10.6 41.9 %collective-permute-start.2 = (bf16[256,1280]{0,1:T(8,128)(2,1)}, bf16[256,1280]{0,1:T(8,128)(2,1)}, u32[]{:S(2)}, u32[]{:S(2)}) collective-permute-start(bf16[256,1280]{0,1:T(8,128)(2,1)} %copy.46), channel_id=1, source_target_pairs={{0,24},{8,0},{16,8},{24,16},{1,25},{9,1},{17,9},{25,17},{2,26},{10... | collective-permute-start | bytes 1966088 | tf_op jit(solution)/shard_map/ppermute | solution.py:24
  13.9 11.8 %copy-start.17 = (bf16[256,1280]{1,0:T(8,128)(2,1)S(1)}, bf16[256,1280]{1,0:T(8,128)(2,1)}, u32[]{:S(2)}) copy-start(bf16[256,1280]{1,0:T(8,128)(2,1)} %param.19) | copy-start | bytes 1966084
  14.1 12.9 %copy-start.1 = (bf16[256,1280]{0,1:T(8,128)(2,1)}, bf16[256,1280]{0,1:T(8,128)(2,1)S(1)}, u32[]{:S(2)}) copy-start(bf16[256,1280]{0,1:T(8,128)(2,1)S(1)} %copy.39) | copy-start | bytes 1966084
  19.8 6.9 %collective-permute-start = (f32[2,256]{1,0:T(2,128)S(1)}, f32[2,256]{1,0:T(2,128)S(1)}, u32[]{:S(2)}, u32[]{:S(2)}) collective-permute-start(f32[2,256]{1,0:T(2,128)S(1)} %pad_maximum_fusion), channel_id=1, source_target_pairs={{4,0},{6,2},{0,4},{2,6},{5,1},{7,3},{1,5},{3,7},{12,8},{14,10},{8,... | collective-permute-start | bytes 6152 | tf_op jit(solution)/shard_map/ppermute | solution.py:34
  27.0 9.3 %copy-start.9 = (bf16[256,1280]{0,1:T(8,128)(2,1)}, bf16[256,1280]{0,1:T(8,128)(2,1)S(1)}, u32[]{:S(2)}) copy-start(bf16[256,1280]{0,1:T(8,128)(2,1)S(1)} %fusion.48) | copy-start | bytes 1966084
  27.3 8.5 %copy-start.3 = (bf16[256,1280]{0,1:T(8,128)(2,1)}, bf16[256,1280]{0,1:T(8,128)(2,1)S(1)}, u32[]{:S(2)}) copy-start(bf16[256,1280]{0,1:T(8,128)(2,1)S(1)} %fusion.40) | copy-start | bytes 1966084
  28.7 23.8 %collective-permute-start.3 = (bf16[256,1280]{0,1:T(8,128)(2,1)}, bf16[256,1280]{0,1:T(8,128)(2,1)}, u32[]{:S(2)}, u32[]{:S(2)}) collective-permute-start(bf16[256,1280]{0,1:T(8,128)(2,1)} %collective-permute-done.1), channel_id=1, source_target_pairs={{0,8},{8,16},{16,24},{24,0},{1,9},{9,17},{17,25},{25,1},{2,10},{10... | collective-permute-start | bytes 1966088 | tf_op jit(solution)/shard_map/ppermute | solution.py:21
  35.8 1.1 copy-start.7
  55.5 2.8 %copy-start.6 = (bf16[256,1280]{0,1:T(8,128)(2,1)S(1)}, bf16[256,1280]{0,1:T(8,128)(2,1)}, u32[]{:S(2)}) copy-start(bf16[256,1280]{0,1:T(8,128)(2,1)} %copy.52) | copy-start | bytes 1966084
  55.5 2.8 %copy-start.8 = (bf16[256,1280]{0,1:T(8,128)(2,1)S(1)}, bf16[256,1280]{0,1:T(8,128)(2,1)}, u32[]{:S(2)}) copy-start(bf16[256,1280]{0,1:T(8,128)(2,1)} %copy.42) | copy-start | bytes 1966084
  58.3 1.1 copy-start.10
  59.4 1.4 copy-start.4
  76.2 2.1 %copy-start.5 = (f32[10,128,256]{2,1,0:T(8,128)S(1)}, f32[10,128,256]{2,1,0:T(8,128)}, u32[]{:S(2)}) copy-start(f32[10,128,256]{2,1,0:T(8,128)} %convolution_multiply_fusion) | copy-start | bytes 3932164
  76.2 86.0 %copy-start.14 = (bf16[10,256,128]{1,2,0:T(8,128)(2,1)S(1)}, bf16[10,256,128]{1,2,0:T(8,128)(2,1)}, u32[]{:S(2)}) copy-start(bf16[10,256,128]{1,2,0:T(8,128)(2,1)} %get-tuple-element.438) | copy-start | bytes 1966084
  78.3 85.0 %copy-start.2 = (bf16[256,1280]{0,1:T(8,128)(2,1)S(1)}, bf16[256,1280]{0,1:T(8,128)(2,1)}, u32[]{:S(2)}) copy-start(bf16[256,1280]{0,1:T(8,128)(2,1)} %copy-done.1) | copy-start | bytes 1966084
  85.1 78.2 %collective-permute-start.4 = (f32[2,256]{1,0:T(2,128)S(1)}, f32[2,256]{1,0:T(2,128)S(1)}, u32[]{:S(2)}, u32[]{:S(2)}) collective-permute-start(f32[2,256]{1,0:T(2,128)S(1)} %pad_maximum_fusion.1), channel_id=1, source_target_pairs={{4,0},{6,2},{0,4},{2,6},{5,1},{7,3},{1,5},{3,7},{12,8},{14,10},{8,... | collective-permute-start | bytes 6152 | tf_op jit(solution)/shard_map/ppermute | solution.py:34
Sparse Core Ops, SparseCore 0:
  9.5 38.4 all-gather.2
  50.1 26.0 all-gather.4
